TPU v7x, 32 devices: a whole 2x2x4 slice. The times are simulated.
32 devices in a mesh: grp: 4 (over y, x), dev: 8 (over z, core).
Axes of the slice: x: 2, y: 2, z: 4, core: 2. Of those that a mesh axis runs over, the one named last changes fastest.
Arguments:
- examples: float32 [2048, 32768], P(('grp', 'dev'))
- labels: int32 [2048], P(('grp', 'dev')), may hold values from 0 to 1, as said below
Outputs:
- consensus: float32 [32768], replicated
- local_weights: float32 [32, 32768], P(('grp', 'dev'))
- dual_vars: float32 [32, 32768], P(('grp', 'dev'))
Inputs may be any that keep to these rules, and one draw needn't show every extreme that they name: `labels`: each example's class, 0 or 1.
All inputs are finite; a program needn't handle non-finite values.
Results may differ from a plain program's by a relative error of at most 0.00012.
Values sent between devices are 32-bit elements; how exact they have to be, the bound alone decides.
A program may use at most 64 MiB of HBM per device.

v0:
```python
import jax
import jax.numpy as jnp
from jax import lax
from jax.sharding import PartitionSpec as P

PROX = 3
ROUNDS = 4
step_size = 200.0
penalty = 0.005
thresh = 0.04


def shrink(values):
    return values - jnp.clip(values, -thresh, thresh)


def local_steps(examples, targets, weight_vector, consensus_point):
    for prox_index in range(PROX):
        label_margins = jnp.dot(examples, weight_vector, precision=lax.Precision.HIGHEST)
        primal_residual = jax.nn.sigmoid(label_margins) - targets
        loss_gradient = jnp.dot(primal_residual, examples, precision=lax.Precision.HIGHEST)
        weight_vector = (
            weight_vector - step_size * loss_gradient + step_size * penalty * consensus_point
        ) / (1.0 + step_size * penalty)
    return weight_vector


def per_device(examples, labels):
    members = lax.axis_size("grp") * lax.axis_size("dev")
    targets = labels.astype(jnp.float32)
    width = examples.shape[1]

    def one_round(round_index, carried):
        consensus, weight_vector, dual_vars = carried
        consensus_point = consensus - dual_vars
        weight_vector = local_steps(examples, targets, weight_vector, consensus_point)
        combined = weight_vector + dual_vars
        summed = lax.psum(combined, ("grp", "dev"))
        consensus = shrink(summed / members)
        dual_vars = dual_vars + weight_vector - consensus
        return (consensus, weight_vector, dual_vars)

    start = (
        jnp.zeros((width,), jnp.float32),
        jnp.zeros((width,), jnp.float32),
        jnp.zeros((width,), jnp.float32),
    )
    consensus, weight_vector, dual_vars = lax.fori_loop(0, ROUNDS, one_round, start)
    return (consensus, weight_vector[None, :], dual_vars[None, :])


def solution(mesh):
    placed = (P(("grp", "dev"), None), P(("grp", "dev")))
    return jax.shard_map(
        per_device,
        mesh=mesh,
        in_specs=placed,
        out_specs=(P(), P(("grp", "dev"), None), P(("grp", "dev"), None)),
        check_vma=False,
    )
```

profile of v0, /device:TPU:0, one launch (start us, length us, event | category | flops | bytes accessed | tf_op | source)
XLA Modules:
  0.0 658.6 jit_solution(14624794344501646285)
XLA Ops:
  7.2 0.7 convert_element_type.3
  7.8 643.4 %while.15 = (s32[]{:T(128)}, f32[32768]{0:T(1024)S(1)}, f32[32768]{0:T(1024)S(1)}, f32[32768]{0:T(1024)S(1)}, f32[64,32768]{1,0:T(8,128)}, /*index=5*/f32[64]{0:T(128)S(1)}, s32[]{:T(128)}, s32[]{:T(128)}) while((s32[]{:T(128)}, f32[32768]{0:T(1024)S(1)}, f32[32768]{0:T(1024)S(1)}, f32[32768]{0:T(1024)S(1)}, ...), condition=%wide.region_2.3_spmd.clone, body=%wide.region_0.2_spmd.clone.sunk | while | flops 151782144 | bytes 88344992 | solution.py:48
  7.9 9.1 %fusion.65 = f32[64,1]{0,1:T(1,128)S(1)} fusion(f32[64]{0:T(128)S(1)} %get-tuple-element.149, f32[64,32768]{1,0:T(8,128)} %get-tuple-element.148, f32[32768,1]{0,1:T(1,128)S(1)} %bitcast.118), kind=kOutput, calls=%fused_computation.20.clone.1 | convolution fusion | flops 25166080 | bytes 8520192 | tf_op jit(solution)/shard_map/while/body/eval_jaxpr/dot_general | solution.py:19
  16.9 4.0 fusion.66
  21.0 6.6 fusion.67
  27.6 4.1 fusion.68
  31.7 6.6 fusion.69
  38.3 4.1 fusion.70
  42.3 0.7 select_add_fusion.2
  43.0 0.0 all-reduce.2.cloned.1.call-update
  43.0 127.3 %all-reduce.2.cloned.1.call-done = f32[32768]{0:T(1024)} async-done(((f32[32768]{0:T(1024)}), f32[32768]{0:T(1024)}) %all-reduce.2.cloned.1.call-update) | async-done | bytes 131088 | tf_op jit(solution)/shard_map/while/body/eval_jaxpr/psum | solution.py:38
  170.4 1.0 fusion.71
  171.4 0.0 all-reduce.2.cloned.1.call-start
  171.5 9.1 %fusion.65 = f32[64,1]{0,1:T(1,128)S(1)} fusion(f32[64]{0:T(128)S(1)} %get-tuple-element.149, f32[64,32768]{1,0:T(8,128)} %get-tuple-element.148, f32[32768,1]{0,1:T(1,128)S(1)} %bitcast.118), kind=kOutput, calls=%fused_computation.20.clone.1 | convolution fusion | flops 25166080 | bytes 8520192 | tf_op jit(solution)/shard_map/while/body/eval_jaxpr/dot_general | solution.py:19
  180.5 4.0 fusion.66
  184.6 6.6 fusion.67
  191.2 4.1 fusion.68
  195.3 6.6 fusion.69
  201.9 4.1 fusion.70
  205.9 0.7 select_add_fusion.2
  206.6 0.0 all-reduce.2.cloned.1.call-update
  206.6 123.7 %all-reduce.2.cloned.1.call-done = f32[32768]{0:T(1024)} async-done(((f32[32768]{0:T(1024)}), f32[32768]{0:T(1024)}) %all-reduce.2.cloned.1.call-update) | async-done | bytes 131088 | tf_op jit(solution)/shard_map/while/body/eval_jaxpr/psum | solution.py:38
  330.3 1.0 fusion.71
  331.3 0.0 all-reduce.2.cloned.1.call-start
  331.4 9.1 %fusion.65 = f32[64,1]{0,1:T(1,128)S(1)} fusion(f32[64]{0:T(128)S(1)} %get-tuple-element.149, f32[64,32768]{1,0:T(8,128)} %get-tuple-element.148, f32[32768,1]{0,1:T(1,128)S(1)} %bitcast.118), kind=kOutput, calls=%fused_computation.20.clone.1 | convolution fusion | flops 25166080 | bytes 8520192 | tf_op jit(solution)/shard_map/while/body/eval_jaxpr/dot_general | solution.py:19
  340.5 4.0 fusion.66
  344.6 6.6 fusion.67
  351.2 4.1 fusion.68
  355.3 6.6 fusion.69
  361.8 4.1 fusion.70
  365.9 0.7 select_add_fusion.2
  366.6 0.0 all-reduce.2.cloned.1.call-update
  366.6 123.7 %all-reduce.2.cloned.1.call-done = f32[32768]{0:T(1024)} async-done(((f32[32768]{0:T(1024)}), f32[32768]{0:T(1024)}) %all-reduce.2.cloned.1.call-update) | async-done | bytes 131088 | tf_op jit(solution)/shard_map/while/body/eval_jaxpr/psum | solution.py:38
  490.3 1.0 fusion.71
  491.3 0.0 all-reduce.2.cloned.1.call-start
  491.4 9.1 %fusion.65 = f32[64,1]{0,1:T(1,128)S(1)} fusion(f32[64]{0:T(128)S(1)} %get-tuple-element.149, f32[64,32768]{1,0:T(8,128)} %get-tuple-element.148, f32[32768,1]{0,1:T(1,128)S(1)} %bitcast.118), kind=kOutput, calls=%fused_computation.20.clone.1 | convolution fusion | flops 25166080 | bytes 8520192 | tf_op jit(solution)/shard_map/while/body/eval_jaxpr/dot_general | solution.py:19
  500.5 4.0 fusion.66
  504.6 6.6 fusion.67
  511.1 4.1 fusion.68
  515.2 6.6 fusion.69
  521.8 4.1 fusion.70
  525.9 0.7 select_add_fusion.2
  526.6 0.0 all-reduce.2.cloned.1.call-update
  526.6 123.7 %all-reduce.2.cloned.1.call-done = f32[32768]{0:T(1024)} async-done(((f32[32768]{0:T(1024)}), f32[32768]{0:T(1024)}) %all-reduce.2.cloned.1.call-update) | async-done | bytes 131088 | tf_op jit(solution)/shard_map/while/body/eval_jaxpr/psum | solution.py:38
  650.3 1.0 fusion.71
  651.3 0.6 copy-done.1
  651.9 0.0 copy-done.2
  652.0 0.0 copy-done.3
  (27 shorter events, 0.4 us)
Async XLA Ops:
  7.8 162.5 %all-reduce.2.cloned.1.call-start = ((), (), s32[]{:S(2)}) async-start(), calls=%async_computation | async-start | bytes 262144 | tf_op jit(solution)/shard_map/while/body/eval_jaxpr/psum | solution.py:38
  7.8 9.1 %copy-start = (f32[64,32768]{1,0:T(8,128)S(1)}, f32[64,32768]{1,0:T(8,128)}, u32[]{:S(2)}) copy-start(f32[64,32768]{1,0:T(8,128)} %get-tuple-element.148) | copy-start | bytes 25165828 | tf_op jit(solution)/shard_map/while
  171.4 159.0 %all-reduce.2.cloned.1.call-start = ((), (), s32[]{:S(2)}) async-start(), calls=%async_computation | async-start | bytes 262144 | tf_op jit(solution)/shard_map/while/body/eval_jaxpr/psum | solution.py:38
  171.4 9.1 %copy-start = (f32[64,32768]{1,0:T(8,128)S(1)}, f32[64,32768]{1,0:T(8,128)}, u32[]{:S(2)}) copy-start(f32[64,32768]{1,0:T(8,128)} %get-tuple-element.148) | copy-start | bytes 25165828 | tf_op jit(solution)/shard_map/while
  331.3 159.0 %all-reduce.2.cloned.1.call-start = ((), (), s32[]{:S(2)}) async-start(), calls=%async_computation | async-start | bytes 262144 | tf_op jit(solution)/shard_map/while/body/eval_jaxpr/psum | solution.py:38
  331.4 9.1 %copy-start = (f32[64,32768]{1,0:T(8,128)S(1)}, f32[64,32768]{1,0:T(8,128)}, u32[]{:S(2)}) copy-start(f32[64,32768]{1,0:T(8,128)} %get-tuple-element.148) | copy-start | bytes 25165828 | tf_op jit(solution)/shard_map/while
  491.3 159.0 %all-reduce.2.cloned.1.call-start = ((), (), s32[]{:S(2)}) async-start(), calls=%async_computation | async-start | bytes 262144 | tf_op jit(solution)/shard_map/while/body/eval_jaxpr/psum | solution.py:38
  491.4 9.1 %copy-start = (f32[64,32768]{1,0:T(8,128)S(1)}, f32[64,32768]{1,0:T(8,128)}, u32[]{:S(2)}) copy-start(f32[64,32768]{1,0:T(8,128)} %get-tuple-element.148) | copy-start | bytes 25165828 | tf_op jit(solution)/shard_map/while
  651.3 0.7 copy-start.1
  651.3 0.7 copy-start.2
  651.3 0.7 copy-start.3
Sparse Core Ops, SparseCore 0:
  43.2 127.1 all-reduce.1
  206.8 123.5 all-reduce.1
  366.7 123.5 all-reduce.1
  526.7 123.5 all-reduce.1
where the time goes:
time: 659 us
  waiting for transfers between devices  498 us (76%)
  matrix products  137 us (21%)
  between operations  13.7 us (2%)
  other arithmetic  7.74 us (1%)
    psum x4, waiting for transfers between devices, one_round(): summed = lax.psum(combined, ('grp', 'dev'))  498 us
    dot_general x12, matrix products, local_steps(): jnp.dot(examples, weight_vector, precision=lax.Precision.HIGHEST)  88.9 us
    dot_general x12, matrix products, local_steps(): jnp.dot(primal_residual, examples, precision=lax.Precision.HIGHEST)  48.6 us
  transfers between devices with their start and end apart: 4, of which 4 were waited for; matrix products, arithmetic and copies ran while one was open for 0% of the time, Pallas kernels for 0%

commit v1 on v0

--- a/solution.py
+++ b/solution.py
@@ -1,3 +1,4 @@
+import functools
 import jax
 import jax.numpy as jnp
 from jax import lax
@@ -8,6 +9,15 @@
 step_size = 200.0
 penalty = 0.005
 thresh = 0.04
+
+
+def gates_save(shard_in, along_axis, bus_axis):
+    for hop_no in (along_axis, bus_axis):
+        shard_in = lax.psum(shard_in, hop_no)
+    return shard_in
+
+
+place_the_entries = functools.partial(gates_save, along_axis="dev", bus_axis="grp")
 
 
 def shrink(values):
@@ -35,7 +45,7 @@
         consensus_point = consensus - dual_vars
         weight_vector = local_steps(examples, targets, weight_vector, consensus_point)
         combined = weight_vector + dual_vars
-        summed = lax.psum(combined, ("grp", "dev"))
+        summed = place_the_entries(combined)
         consensus = shrink(summed / members)
         dual_vars = dual_vars + weight_vector - consensus
         return (consensus, weight_vector, dual_vars)

time: 659 us -> 560 us (0.85)
  waiting for transfers between devices: 498 us -> 399 us
    psum x4 -> x8, waiting for transfers between devices: 498 us -> 399 us  [gates_save(): shard_in = lax.psum(shard_in, hop_no)]
  transfers between devices with their start and end apart: 4 -> 8, of which waited for: 4 -> 8; matrix products, arithmetic and copies ran while one was open for 0% -> 0% of each run, Pallas kernels for 0% -> 0%
where the time goes in v1:
time: 560 us
  waiting for transfers between devices  399 us (71%)
  matrix products  137 us (24%)
  between operations  14 us (2%)
  other arithmetic  7.75 us (1%)
    psum x8, waiting for transfers between devices, gates_save(): shard_in = lax.psum(shard_in, hop_no)  399 us
    dot_general x12, matrix products, local_steps(): jnp.dot(examples, weight_vector, precision=lax.Precision.HIGHEST)  88.9 us
    dot_general x12, matrix products, local_steps(): jnp.dot(primal_residual, examples, precision=lax.Precision.HIGHEST)  48.6 us
  transfers between devices with their start and end apart: 8, of which 8 were waited for; matrix products, arithmetic and copies ran while one was open for 0% of the time, Pallas kernels for 0%

profile of v1, /device:TPU:0, one launch (start us, length us, event | category | flops | bytes accessed | tf_op | source)
XLA Modules:
  0.0 559.9 jit_solution(9906690326476025602)
XLA Ops:
  7.2 0.7 convert_element_type.3
  7.8 544.5 %while.15 = (s32[]{:T(128)}, f32[32768]{0:T(1024)S(1)}, f32[32768]{0:T(1024)S(1)}, f32[32768]{0:T(1024)S(1)}, f32[64,32768]{1,0:T(8,128)}, /*index=5*/f32[64]{0:T(128)S(1)}, s32[]{:T(128)}, s32[]{:T(128)}) while((s32[]{:T(128)}, f32[32768]{0:T(1024)S(1)}, f32[32768]{0:T(1024)S(1)}, f32[32768]{0:T(1024)S(1)}, ...), condition=%wide.region_3.4_spmd.clone, body=%wide.region_0.3_spmd.clone.sunk | while | flops 151814912 | bytes 89131464 | solution.py:58
  7.9 9.1 %fusion.65 = f32[64,1]{0,1:T(1,128)S(1)} fusion(f32[64]{0:T(128)S(1)} %get-tuple-element.149, f32[64,32768]{1,0:T(8,128)} %get-tuple-element.148, f32[32768,1]{0,1:T(1,128)S(1)} %bitcast.118), kind=kOutput, calls=%fused_computation.20.clone.1 | convolution fusion | flops 25166080 | bytes 8520192 | tf_op jit(solution)/shard_map/while/body/eval_jaxpr/dot_general | solution.py:29
  16.9 4.0 fusion.66
  21.0 6.6 %fusion.67 = f32[64,1]{0,1:T(1,128)S(1)} fusion(f32[64]{0:T(128)S(1)} %get-tuple-element.149, f32[32768,1]{0,1:T(1,128)S(1)} %bitcast.117, f32[64,32768]{1,0:T(8,128)S(1)} %copy-done), kind=kOutput, calls=%fused_computation.13.clone.1 | convolution fusion | flops 25166080 | bytes 8520192 | tf_op jit(solution)/shard_map/while/body/eval_jaxpr/dot_general | solution.py:29
  27.6 4.1 fusion.68
  31.7 6.6 %fusion.69 = f32[64,1]{0,1:T(1,128)S(1)} fusion(f32[64]{0:T(128)S(1)} %get-tuple-element.149, f32[32768,1]{0,1:T(1,128)S(1)} %bitcast.116, f32[64,32768]{1,0:T(8,128)S(1)} %copy-done), kind=kOutput, calls=%fused_computation.6.clone.1 | convolution fusion | flops 25166080 | bytes 8520192 | tf_op jit(solution)/shard_map/while/body/eval_jaxpr/dot_general | solution.py:29
  38.3 4.1 fusion.70
  42.3 0.7 select_add_fusion.2
  43.1 57.8 %all-reduce.3.cloned.1.call-done = f32[32768]{0:T(1024)} async-done(((f32[32768]{0:T(1024)}), f32[32768]{0:T(1024)}) %all-reduce.3.cloned.1.call-update) | async-done | bytes 131088 | tf_op jit(solution)/shard_map/while/body/eval_jaxpr/psum | solution.py:16
  100.9 44.2 %all-reduce.5.cloned.1.call-done = f32[32768]{0:T(1024)} async-done(((f32[32768]{0:T(1024)}), f32[32768]{0:T(1024)}) %all-reduce.5.cloned.1.call-update) | async-done | bytes 131088 | tf_op jit(solution)/shard_map/while/body/eval_jaxpr/psum | solution.py:16
  145.0 1.0 fusion.71
  146.0 0.0 all-reduce.3.cloned.1.call-start
  146.1 9.1 %fusion.65 = f32[64,1]{0,1:T(1,128)S(1)} fusion(f32[64]{0:T(128)S(1)} %get-tuple-element.149, f32[64,32768]{1,0:T(8,128)} %get-tuple-element.148, f32[32768,1]{0,1:T(1,128)S(1)} %bitcast.118), kind=kOutput, calls=%fused_computation.20.clone.1 | convolution fusion | flops 25166080 | bytes 8520192 | tf_op jit(solution)/shard_map/while/body/eval_jaxpr/dot_general | solution.py:29
  155.2 4.0 fusion.66
  159.3 6.6 %fusion.67 = f32[64,1]{0,1:T(1,128)S(1)} fusion(f32[64]{0:T(128)S(1)} %get-tuple-element.149, f32[32768,1]{0,1:T(1,128)S(1)} %bitcast.117, f32[64,32768]{1,0:T(8,128)S(1)} %copy-done), kind=kOutput, calls=%fused_computation.13.clone.1 | convolution fusion | flops 25166080 | bytes 8520192 | tf_op jit(solution)/shard_map/while/body/eval_jaxpr/dot_general | solution.py:29
  165.9 4.1 fusion.68
  170.0 6.6 %fusion.69 = f32[64,1]{0,1:T(1,128)S(1)} fusion(f32[64]{0:T(128)S(1)} %get-tuple-element.149, f32[32768,1]{0,1:T(1,128)S(1)} %bitcast.116, f32[64,32768]{1,0:T(8,128)S(1)} %copy-done), kind=kOutput, calls=%fused_computation.6.clone.1 | convolution fusion | flops 25166080 | bytes 8520192 | tf_op jit(solution)/shard_map/while/body/eval_jaxpr/dot_general | solution.py:29
  176.6 4.1 fusion.70
  180.6 0.7 select_add_fusion.2
  181.4 55.0 %all-reduce.3.cloned.1.call-done = f32[32768]{0:T(1024)} async-done(((f32[32768]{0:T(1024)}), f32[32768]{0:T(1024)}) %all-reduce.3.cloned.1.call-update) | async-done | bytes 131088 | tf_op jit(solution)/shard_map/while/body/eval_jaxpr/psum | solution.py:16
  236.4 44.0 %all-reduce.5.cloned.1.call-done = f32[32768]{0:T(1024)} async-done(((f32[32768]{0:T(1024)}), f32[32768]{0:T(1024)}) %all-reduce.5.cloned.1.call-update) | async-done | bytes 131088 | tf_op jit(solution)/shard_map/while/body/eval_jaxpr/psum | solution.py:16
  280.4 1.0 fusion.71
  281.4 0.0 all-reduce.3.cloned.1.call-start
  281.5 9.1 %fusion.65 = f32[64,1]{0,1:T(1,128)S(1)} fusion(f32[64]{0:T(128)S(1)} %get-tuple-element.149, f32[64,32768]{1,0:T(8,128)} %get-tuple-element.148, f32[32768,1]{0,1:T(1,128)S(1)} %bitcast.118), kind=kOutput, calls=%fused_computation.20.clone.1 | convolution fusion | flops 25166080 | bytes 8520192 | tf_op jit(solution)/shard_map/while/body/eval_jaxpr/dot_general | solution.py:29
  290.6 4.0 fusion.66
  294.7 6.6 %fusion.67 = f32[64,1]{0,1:T(1,128)S(1)} fusion(f32[64]{0:T(128)S(1)} %get-tuple-element.149, f32[32768,1]{0,1:T(1,128)S(1)} %bitcast.117, f32[64,32768]{1,0:T(8,128)S(1)} %copy-done), kind=kOutput, calls=%fused_computation.13.clone.1 | convolution fusion | flops 25166080 | bytes 8520192 | tf_op jit(solution)/shard_map/while/body/eval_jaxpr/dot_general | solution.py:29
  301.3 4.1 fusion.68
  305.3 6.6 %fusion.69 = f32[64,1]{0,1:T(1,128)S(1)} fusion(f32[64]{0:T(128)S(1)} %get-tuple-element.149, f32[32768,1]{0,1:T(1,128)S(1)} %bitcast.116, f32[64,32768]{1,0:T(8,128)S(1)} %copy-done), kind=kOutput, calls=%fused_computation.6.clone.1 | convolution fusion | flops 25166080 | bytes 8520192 | tf_op jit(solution)/shard_map/while/body/eval_jaxpr/dot_general | solution.py:29
  311.9 4.1 fusion.70
  316.0 0.7 select_add_fusion.2
  316.7 55.0 %all-reduce.3.cloned.1.call-done = f32[32768]{0:T(1024)} async-done(((f32[32768]{0:T(1024)}), f32[32768]{0:T(1024)}) %all-reduce.3.cloned.1.call-update) | async-done | bytes 131088 | tf_op jit(solution)/shard_map/while/body/eval_jaxpr/psum | solution.py:16
  371.8 44.0 %all-reduce.5.cloned.1.call-done = f32[32768]{0:T(1024)} async-done(((f32[32768]{0:T(1024)}), f32[32768]{0:T(1024)}) %all-reduce.5.cloned.1.call-update) | async-done | bytes 131088 | tf_op jit(solution)/shard_map/while/body/eval_jaxpr/psum | solution.py:16
  415.8 1.0 fusion.71
  416.8 0.0 all-reduce.3.cloned.1.call-start
  416.9 9.1 %fusion.65 = f32[64,1]{0,1:T(1,128)S(1)} fusion(f32[64]{0:T(128)S(1)} %get-tuple-element.149, f32[64,32768]{1,0:T(8,128)} %get-tuple-element.148, f32[32768,1]{0,1:T(1,128)S(1)} %bitcast.118), kind=kOutput, calls=%fused_computation.20.clone.1 | convolution fusion | flops 25166080 | bytes 8520192 | tf_op jit(solution)/shard_map/while/body/eval_jaxpr/dot_general | solution.py:29
  426.0 4.0 fusion.66
  430.0 6.6 %fusion.67 = f32[64,1]{0,1:T(1,128)S(1)} fusion(f32[64]{0:T(128)S(1)} %get-tuple-element.149, f32[32768,1]{0,1:T(1,128)S(1)} %bitcast.117, f32[64,32768]{1,0:T(8,128)S(1)} %copy-done), kind=kOutput, calls=%fused_computation.13.clone.1 | convolution fusion | flops 25166080 | bytes 8520192 | tf_op jit(solution)/shard_map/while/body/eval_jaxpr/dot_general | solution.py:29
  436.6 4.1 fusion.68
  440.7 6.6 %fusion.69 = f32[64,1]{0,1:T(1,128)S(1)} fusion(f32[64]{0:T(128)S(1)} %get-tuple-element.149, f32[32768,1]{0,1:T(1,128)S(1)} %bitcast.116, f32[64,32768]{1,0:T(8,128)S(1)} %copy-done), kind=kOutput, calls=%fused_computation.6.clone.1 | convolution fusion | flops 25166080 | bytes 8520192 | tf_op jit(solution)/shard_map/while/body/eval_jaxpr/dot_general | solution.py:29
  447.3 4.1 fusion.70
  451.3 0.7 select_add_fusion.2
  452.1 55.0 %all-reduce.3.cloned.1.call-done = f32[32768]{0:T(1024)} async-done(((f32[32768]{0:T(1024)}), f32[32768]{0:T(1024)}) %all-reduce.3.cloned.1.call-update) | async-done | bytes 131088 | tf_op jit(solution)/shard_map/while/body/eval_jaxpr/psum | solution.py:16
  507.1 44.2 %all-reduce.5.cloned.1.call-done = f32[32768]{0:T(1024)} async-done(((f32[32768]{0:T(1024)}), f32[32768]{0:T(1024)}) %all-reduce.5.cloned.1.call-update) | async-done | bytes 131088 | tf_op jit(solution)/shard_map/while/body/eval_jaxpr/psum | solution.py:16
  551.3 1.0 fusion.71
  552.3 0.6 copy-done.1
  553.0 0.0 copy-done.2
  553.0 0.0 copy-done.3
  (39 shorter events, 0.7 us)
Async XLA Ops:
  7.8 93.0 %all-reduce.3.cloned.1.call-start = ((), (), s32[]{:S(2)}) async-start(), calls=%async_computation | async-start | bytes 262144 | tf_op jit(solution)/shard_map/while/body/eval_jaxpr/psum | solution.py:16
  7.8 9.1 %copy-start = (f32[64,32768]{1,0:T(8,128)S(1)}, f32[64,32768]{1,0:T(8,128)}, u32[]{:S(2)}) copy-start(f32[64,32768]{1,0:T(8,128)} %get-tuple-element.148) | copy-start | bytes 25165828 | tf_op jit(solution)/shard_map/while
  43.0 102.0 %all-reduce.5.cloned.1.call-start = ((), (), s32[]{:S(2)}) async-start(), calls=%async_computation.1 | async-start | bytes 262144 | tf_op jit(solution)/shard_map/while/body/eval_jaxpr/psum | solution.py:16
  146.0 90.3 %all-reduce.3.cloned.1.call-start = ((), (), s32[]{:S(2)}) async-start(), calls=%async_computation | async-start | bytes 262144 | tf_op jit(solution)/shard_map/while/body/eval_jaxpr/psum | solution.py:16
  146.1 9.1 %copy-start = (f32[64,32768]{1,0:T(8,128)S(1)}, f32[64,32768]{1,0:T(8,128)}, u32[]{:S(2)}) copy-start(f32[64,32768]{1,0:T(8,128)} %get-tuple-element.148) | copy-start | bytes 25165828 | tf_op jit(solution)/shard_map/while
  181.3 99.1 %all-reduce.5.cloned.1.call-start = ((), (), s32[]{:S(2)}) async-start(), calls=%async_computation.1 | async-start | bytes 262144 | tf_op jit(solution)/shard_map/while/body/eval_jaxpr/psum | solution.py:16
  281.4 90.3 %all-reduce.3.cloned.1.call-start = ((), (), s32[]{:S(2)}) async-start(), calls=%async_computation | async-start | bytes 262144 | tf_op jit(solution)/shard_map/while/body/eval_jaxpr/psum | solution.py:16
  281.5 9.1 %copy-start = (f32[64,32768]{1,0:T(8,128)S(1)}, f32[64,32768]{1,0:T(8,128)}, u32[]{:S(2)}) copy-start(f32[64,32768]{1,0:T(8,128)} %get-tuple-element.148) | copy-start | bytes 25165828 | tf_op jit(solution)/shard_map/while
  316.7 99.1 %all-reduce.5.cloned.1.call-start = ((), (), s32[]{:S(2)}) async-start(), calls=%async_computation.1 | async-start | bytes 262144 | tf_op jit(solution)/shard_map/while/body/eval_jaxpr/psum | solution.py:16
  416.8 90.3 %all-reduce.3.cloned.1.call-start = ((), (), s32[]{:S(2)}) async-start(), calls=%async_computation | async-start | bytes 262144 | tf_op jit(solution)/shard_map/while/body/eval_jaxpr/psum | solution.py:16
  416.8 9.1 %copy-start = (f32[64,32768]{1,0:T(8,128)S(1)}, f32[64,32768]{1,0:T(8,128)}, u32[]{:S(2)}) copy-start(f32[64,32768]{1,0:T(8,128)} %get-tuple-element.148) | copy-start | bytes 25165828 | tf_op jit(solution)/shard_map/while
  452.1 99.2 %all-reduce.5.cloned.1.call-start = ((), (), s32[]{:S(2)}) async-start(), calls=%async_computation.1 | async-start | bytes 262144 | tf_op jit(solution)/shard_map/while/body/eval_jaxpr/psum | solution.py:16
  552.3 0.7 copy-start.1
  552.3 0.7 copy-start.2
  552.3 0.7 copy-start.3
Sparse Core Ops, SparseCore 0:
  43.2 57.6 all-reduce.2
  103.7 41.2 all-reduce.4
  181.4 54.8 all-reduce.2
  239.1 41.2 all-reduce.4
  316.8 54.8 all-reduce.2
  374.5 41.2 all-reduce.4
  452.2 54.8 all-reduce.2
  510.0 41.2 all-reduce.4
